TPU v7x, 128 devices: a whole 4x4x4 slice. The times are simulated.
128 devices in a mesh: dp: 16 (over x_lo, z, core), expert: 8 (over y, x_hi).
Axes of the slice: x: 4 (x_hi: 2, x_lo: 2; x = x_hi * 2 + x_lo), y: 4, z: 4, core: 2. Of those that a mesh axis runs over, the one named last changes fastest.
Arguments:
- tokens: bfloat16 [16384, 2048], P(('dp', 'expert')), may hold values from -6 to 6
- norm_gain: float32 [2048], replicated, may hold values from 0.25 to 1.75
- router_weight: bfloat16 [2048, 64], P('dp'), may hold values from -0.25 to 0.25
- expert_ids: int32 [16384, 8], P(('dp', 'expert')), may hold values from 0 to 63, all different within a row; in each aligned block of 128 rows (0 to 127, 128 to 255, ...) at most 32 rows name the same one
- gate_weight: bfloat16 [8, 2048, 1024], P('expert', 'dp'), may hold values from -0.125 to 0.125
- up_weight: bfloat16 [8, 2048, 1024], P('expert', 'dp'), may hold values from -0.125 to 0.125
- down_weight: bfloat16 [8, 2048, 1024], P('expert', 'dp'), may hold values from -0.1875 to 0.1875
- cotangent: bfloat16 [16384, 2048], P(('dp', 'expert')), may hold values from -6 to 6
Outputs:
- mixed: bfloat16 [16384, 2048], P(('dp', 'expert'))
- d_tokens: bfloat16 [16384, 2048], P(('dp', 'expert'))
- d_gain: float32 [2048], replicated
- d_router: float32 [2048, 64], P('dp')
- d_gate: bfloat16 [8, 2048, 1024], P('expert', 'dp')
- d_up: bfloat16 [8, 2048, 1024], P('expert', 'dp')
- d_down: bfloat16 [8, 2048, 1024], P('expert', 'dp')
Inputs may be any that keep to these rules, and one draw needn't show every extreme that they name: `expert_ids`: each row names 8 different experts; in the rows of one device no expert is named more than 32 times.
All inputs are finite; a program needn't handle non-finite values.
Results may differ from a plain program's by a relative error of at most 0.018.
Values may be sent and summed in bfloat16 or wider, within the bound.
No kernel may reach another device: no remote copies, remote signals or barrier semaphores. Data moves between devices by JAX's collectives and lax.ppermute only.
A program may use at most 128 MiB of HBM per device.

v0:
```python
import jax
import jax.numpy as jnp
from jax import lax
from jax.sharding import PartitionSpec as P

D = 2048
FF = 1024
CAP = 32
EPSILON = 1e-05
HIGHEST = lax.Precision.HIGHEST


def in_one_piece(arrays, axis, dim, along):
    both = jnp.concatenate(arrays, axis=along)
    result, at, finished = (lax.all_gather(both, axis, axis=dim, tiled=True), 0, [])
    for a in arrays:
        finished.append(lax.slice_in_dim(result, at, at + a.shape[along], axis=along))
        at += a.shape[along]
    return tuple(finished)


def split_up(x, dim, length):
    shape = x.shape
    pieces = x.reshape(*shape[:dim], length, shape[dim] // length, *shape[dim + 1 :])
    return jnp.moveaxis(pieces, dim, 0)


def sum_at_owner(x, axis, dim):
    length = lax.axis_size(axis)
    pieces = lax.all_to_all(split_up(x, dim, length), axis, 0, 0, tiled=True)
    return jnp.sum(pieces.astype(jnp.float32), axis=0)


def copy_for_each(x, axis):
    copies = jnp.broadcast_to(x, (lax.axis_size(axis), *x.shape))
    return lax.all_to_all(copies, axis, split_axis=0, concat_axis=0, tiled=True)


def over_copies(x, axis):
    everything = copy_for_each(x, axis)
    return jnp.sum(everything.astype(jnp.float32), axis=0)


def normalize(inputs, norm_gain):
    meansq = jnp.mean(inputs * inputs, axis=-1, keepdims=True)
    return inputs * lax.rsqrt(meansq + EPSILON) * norm_gain


def gate_weights(logits, expert_ids):
    member = (
        expert_ids[:, :, None] == jnp.arange(logits.shape[-1], dtype=jnp.int32)[None, None, :]
    ).astype(jnp.float32)
    picked = jnp.sum(member * logits[:, None, :], axis=-1)
    raised = jnp.exp(picked)
    return raised / jnp.sum(raised, axis=-1, keepdims=True)


def pick_matrix(expert_ids, window, capacity):
    flat_ids = expert_ids.reshape(-1)
    chosen = (flat_ids[:, None] == jnp.arange(window, dtype=jnp.int32)[None, :]).astype(jnp.int32)
    before = jnp.cumsum(chosen, axis=0, dtype=jnp.int32) - chosen
    position = jnp.sum(before * chosen, axis=-1)
    target = jnp.where(flat_ids < window, flat_ids * capacity + position, -1)
    columns = jnp.arange(window * capacity, dtype=jnp.int32)
    matrix = (target[:, None] == columns[None, :]).astype(jnp.float32)
    return matrix.reshape(expert_ids.shape[0], expert_ids.shape[1], window * capacity)


def expert_forward(slot_rows, w_gate, w_up, w_down):
    gate_pre = jnp.dot(slot_rows, w_gate, preferred_element_type=jnp.float32)
    up_pre = jnp.dot(slot_rows, w_up, preferred_element_type=jnp.float32)
    active = (gate_pre * jax.nn.sigmoid(gate_pre) * up_pre).astype(jnp.bfloat16)
    output = jnp.dot(active, w_down.T, preferred_element_type=jnp.float32).astype(jnp.bfloat16)
    return (output, gate_pre, up_pre)


def expert_backward(slot_grads, gate_pre, up_pre, w_gate, w_up, w_down):
    sigmoid_gate = jax.nn.sigmoid(gate_pre)
    active = (gate_pre * sigmoid_gate * up_pre).astype(jnp.bfloat16)
    back = jnp.dot(slot_grads, w_down, preferred_element_type=jnp.float32)
    grad_gate = (back * up_pre * sigmoid_gate * (1.0 + gate_pre * (1.0 - sigmoid_gate))).astype(
        jnp.bfloat16
    )
    grad_upper = (back * gate_pre * sigmoid_gate).astype(jnp.bfloat16)
    grad_rows = jnp.dot(grad_gate, w_gate.T, preferred_element_type=jnp.float32)
    grad_rows = (
        grad_rows + jnp.dot(grad_upper, w_up.T, preferred_element_type=jnp.float32)
    ).astype(jnp.bfloat16)
    return (grad_rows, active, grad_gate, grad_upper)


def body(
    tokens, norm_gain, router_weight, expert_ids, gate_weight, up_weight, down_weight, cotangent
):
    window = lax.axis_size("expert")
    slot_count = window * CAP
    router_full = lax.all_gather(router_weight, "dp", axis=0, tiled=True)
    inputs = tokens.astype(jnp.float32)
    hidden = normalize(inputs, norm_gain).astype(jnp.bfloat16)
    logits = jnp.dot(hidden, router_full, preferred_element_type=jnp.float32)
    weights, gate_back = jax.vjp(lambda values: gate_weights(values, expert_ids), logits)
    pick_table = pick_matrix(expert_ids, window, CAP)
    spread_half = jnp.sum(pick_table, axis=1).astype(jnp.bfloat16)
    blending = jnp.einsum("tks,tk->ts", pick_table, weights, precision=HIGHEST)
    outgoing = (
        jnp.dot(spread_half.T, hidden, preferred_element_type=jnp.float32)
        .astype(jnp.bfloat16)
        .reshape(window, CAP, D)
    )
    weights_full = in_one_piece((gate_weight, up_weight, down_weight), "dp", 1, 0)
    w_gate = weights_full[0][0]
    w_up = weights_full[1][0]
    w_down = weights_full[2][0]
    arrived_rows = lax.all_to_all(outgoing, "expert", split_axis=0, concat_axis=0, tiled=True)
    lead = arrived_rows.shape[0]
    middle = arrived_rows.shape[1]
    output, gate_pre, up_pre = expert_forward(arrived_rows.reshape(-1, D), w_gate, w_up, w_down)
    produced = output.reshape(lead, middle, D)
    gate_slots = gate_pre.reshape(lead, middle, FF)
    upper_slots = up_pre.reshape(lead, middle, FF)
    returned = lax.all_to_all(produced, "expert", split_axis=0, concat_axis=0, tiled=True).reshape(
        slot_count, D
    )
    returned_wide = returned.astype(jnp.float32)
    mixed_out = jnp.dot(blending, returned_wide, precision=HIGHEST).astype(jnp.bfloat16)
    gathered_cot = jnp.dot(spread_half.T, cotangent, preferred_element_type=jnp.float32)
    per_slot = jnp.sum(gathered_cot * returned_wide, axis=-1)
    grad_weights = jnp.einsum("tks,s->tk", pick_table, per_slot, precision=HIGHEST)
    grad_logits = gate_back(grad_weights)[0]
    outgoing_grad = (
        jnp.dot(blending.T, cotangent.astype(jnp.float32), precision=HIGHEST)
        .astype(jnp.bfloat16)
        .reshape(window, CAP, D)
    )
    arrived_grad = lax.all_to_all(outgoing_grad, "expert", split_axis=0, concat_axis=0, tiled=True)
    flat_rows = arrived_rows.reshape(-1, D)
    flat_grads = arrived_grad.reshape(-1, D)
    grad_rows, active, grad_gate, grad_upper = expert_backward(
        flat_grads, gate_slots.reshape(-1, FF), upper_slots.reshape(-1, FF), w_gate, w_up, w_down
    )
    grad_back = lax.all_to_all(
        grad_rows.reshape(window, CAP, D), "expert", split_axis=0, concat_axis=0, tiled=True
    ).reshape(slot_count, D)
    term_gate = jnp.dot(flat_rows.T, grad_gate, preferred_element_type=jnp.float32)
    term_upper = jnp.dot(flat_rows.T, grad_upper, preferred_element_type=jnp.float32)
    term_down = jnp.dot(flat_grads.T, active, preferred_element_type=jnp.float32)
    summed = lax.psum_scatter(
        jnp.concatenate([term_gate, term_upper, term_down], axis=1).astype(jnp.bfloat16),
        "dp",
        scatter_dimension=0,
        tiled=True,
    ).astype(jnp.float32)
    grad_hidden = jnp.dot(spread_half, grad_back, preferred_element_type=jnp.float32)
    grad_hidden = grad_hidden + jnp.dot(
        grad_logits, router_full.astype(jnp.float32).T, precision=HIGHEST
    )
    unused_value, norm_back = jax.vjp(normalize, inputs, norm_gain)
    grad_inputs, grad_gain = norm_back(grad_hidden)
    grad_router = jnp.dot(hidden.astype(jnp.float32).T, grad_logits, precision=HIGHEST)
    router_part = sum_at_owner(grad_router.astype(jnp.bfloat16), "dp", 0)
    router_mine = over_copies(router_part.astype(jnp.bfloat16), "expert").astype(jnp.float32)
    gain_sum = lax.psum(grad_gain, ("dp", "expert"))
    grad_gate_out = summed[:, :FF].astype(jnp.bfloat16)[None]
    grad_up_out = summed[:, FF : 2 * FF].astype(jnp.bfloat16)[None]
    grad_down_out = summed[:, 2 * FF :].astype(jnp.bfloat16)[None]
    return (
        mixed_out,
        grad_inputs.astype(jnp.bfloat16),
        gain_sum,
        router_mine,
        grad_gate_out,
        grad_up_out,
        grad_down_out,
    )


def solution(mesh):
    in_specs = (
        P(("dp", "expert"), None),
        P(),
        P("dp", None),
        P(("dp", "expert"), None),
        P("expert", "dp", None),
        P("expert", "dp", None),
        P("expert", "dp", None),
        P(("dp", "expert"), None),
    )
    out_specs = (
        P(("dp", "expert"), None),
        P(("dp", "expert"), None),
        P(),
        P("dp", None),
        P("expert", "dp", None),
        P("expert", "dp", None),
        P("expert", "dp", None),
    )
    return jax.shard_map(body, mesh=mesh, in_specs=in_specs, out_specs=out_specs, check_vma=False)
```

profile of v0, /device:TPU:1, one launch (start us, length us, event | category | flops | bytes accessed | tf_op | source)
XLA Modules:
  0.0 330.0 jit_solution(3319858266487233548)
XLA Ops:
  7.3 2.2 pad_maximum_fusion.1
  9.5 0.8 copy.56
  10.2 0.1 eq.57
  10.3 0.1 eq.53
  10.4 2.3 reduce-window.6
  12.7 0.3 slice_reduce_fusion
  13.0 0.2 reduce-window.9
  13.2 0.1 add_bitcast_fusion
  13.3 0.1 reduce_sum.114
  13.4 0.7 add_select_fusion
  14.1 0.1 copy.59
  14.2 0.4 convert_reduce_fusion
  14.6 1.2 fusion.16
  15.9 2.5 convolution_convert_fusion.3
  18.4 7.5 %all-to-all-start = ((bf16[8,32,2048]{2,1,0:T(8,128)(2,1)}), bf16[8,32,2048]{2,1,0:T(8,128)(2,1)S(1)}, u32[]{:S(2)}, u32[]{:S(2)}) async-start(bf16[8,32,2048]{2,1,0:T(8,128)(2,1)} %bitcast.3), calls=%async_computation | async-start | bytes 2097152 | tf_op jit(solution)/shard_map/all_to_all | solution.py:114
  25.9 41.0 %all_gather.6 = bf16[2048,64]{0,1:T(8,128)(2,1)S(1)} all-gather(bf16[128,64]{0,1:T(8,128)(2,1)S(1)} %copy-done.14), channel_id=1, replica_groups=mesh['dp'=16,'expert'=8] {'dp'}, dimensions={0}, use_global_device_ids=true | all-gather | bytes 278528 | tf_op jit(solution)/shard_map/all_gather | solution.py:97
  67.0 0.7 copy-done.2
  67.7 0.4 fusion.41
  68.1 0.1 copy.65
  68.2 0.7 fusion.19
  69.0 2.1 convolution_convert_fusion.4
  71.1 6.8 %all-to-all-start.2 = ((bf16[8,32,2048]{2,1,0:T(8,128)(2,1)}), bf16[8,32,2048]{2,1,0:T(8,128)(2,1)S(1)}, u32[]{:S(2)}, u32[]{:S(2)}) async-start(bf16[8,32,2048]{2,1,0:T(8,128)(2,1)} %bitcast.109), calls=%async_computation.2 | async-start | bytes 2097152 | tf_op jit(solution)/shard_map/all_to_all | solution.py:135
  77.9 0.2 reduce-scatter.4.cloned.1.call-start
  78.1 30.4 %all-gather.2.cloned.1.call-done = bf16[3,2048,1024]{2,1,0:T(8,128)(2,1)} async-done(((bf16[3,128,1024]{2,1,0:T(8,128)(2,1)}), bf16[3,2048,1024]{2,1,0:T(8,128)(2,1)}) %all-gather.2.cloned.1.call-update) | async-done | bytes 12582928 | tf_op jit(solution)/shard_map/all_gather | solution.py:15
  108.5 4.4 %fusion.3 = f32[256,1024]{1,0:T(8,128)} fusion(bf16[256,2048]{1,0:T(8,128)(2,1)S(1)} %bitcast.100, bf16[3,2048,1024]{2,1,0:T(8,128)(2,1)} %all-gather.2.cloned.1.call-done), kind=kOutput, calls=%fused_computation.10 | convolution fusion | flops 1073741824 | bytes 6291456 | tf_op jit(solution)/shard_map/dot_general | solution.py:71
  112.9 4.4 %fusion.1 = f32[256,1024]{1,0:T(8,128)} fusion(bf16[256,2048]{1,0:T(8,128)(2,1)S(1)} %bitcast.101, bf16[3,2048,1024]{2,1,0:T(8,128)(2,1)} %all-gather.2.cloned.1.call-done), kind=kOutput, calls=%fused_computation.8 | convolution fusion | flops 1073741824 | bytes 6291456 | tf_op jit(solution)/shard_map/dot_general | solution.py:70
  117.3 4.4 %multiply_convert_fusion = (bf16[256,1024]{1,0:T(8,128)(2,1)S(1)}, bf16[256,1024]{1,0:T(8,128)(2,1)S(1)}, bf16[256,1024]{1,0:T(8,128)(2,1)S(1)}) fusion(f32[256,1024]{1,0:T(8,128)} %fusion.1, f32[256,1024]{1,0:T(8,128)} %fusion.3, bf16[256,2048]{1,0:T(8,128)(2,1)S(1)} %bitcast.104, bf16[3,2048,1024]{2,1,0:T(8,128)(2,1)} %all-gather.2.cloned.1.call-done), kind=kOutput, calls=%fused_computation.36 | convolution fusion | flops 1077936128 | bytes 8912896 | tf_op jit(solution)/shard_map/dot_general | solution.py:80
  121.7 1.3 convolution_convert_fusion
  123.1 1.3 convolution_convert_fusion.1
  124.4 1.3 convolution_convert_fusion.2
  125.7 21.2 %pad_maximum_fusion = bf16[2048,3072]{0,1:T(8,128)(2,1)} fusion(bf16[2048,1024]{0,1:T(8,128)(2,1)S(1)} %convolution_convert_fusion, bf16[2048,1024]{0,1:T(8,128)(2,1)S(1)} %convolution_convert_fusion.1, bf16[2048,1024]{0,1:T(8,128)(2,1)S(1)} %convolution_convert_fusion.2), kind=kLoop, calls=%fused_computation | loop fusion | flops 37748736 | bytes 25165824 | tf_op jit(solution)/shard_map/concatenate | solution.py:148
  146.9 16.6 %copy.68 = bf16[2048,3072]{1,0:T(8,128)(2,1)} copy(bf16[2048,3072]{0,1:T(8,128)(2,1)} %pad_maximum_fusion) | data formatting | bytes 25165824
  163.6 1.0 copy-done.8
  164.6 4.6 %fusion.8 = bf16[256,2048]{1,0:T(8,128)(2,1)} fusion(bf16[256,1024]{1,0:T(8,128)(2,1)S(1)} %copy-done.8, bf16[3,2048,1024]{2,1,0:T(8,128)(2,1)} %all-gather.2.cloned.1.call-done), kind=kOutput, calls=%fused_computation.17 | convolution fusion | flops 1074266112 | bytes 5767168 | tf_op jit(solution)/shard_map/dot_general | solution.py:73
  169.2 6.1 %all-to-all-start.1 = ((bf16[8,32,2048]{2,1,0:T(8,128)(2,1)}), bf16[8,32,2048]{2,1,0:T(8,128)(2,1)S(1)}, u32[]{:S(2)}, u32[]{:S(2)}) async-start(bf16[8,32,2048]{2,1,0:T(8,128)(2,1)} %bitcast.8), calls=%async_computation.1 | async-start | bytes 2097152 | tf_op jit(solution)/shard_map/all_to_all | solution.py:121
  175.3 3.5 %fusion = f32[256,2048]{1,0:T(8,128)S(1)} fusion(bf16[256,1024]{1,0:T(8,128)(2,1)S(1)} %copy-done.6, bf16[3,2048,1024]{2,1,0:T(8,128)(2,1)} %all-gather.2.cloned.1.call-done), kind=kOutput, calls=%fused_computation.7 | convolution fusion | flops 1073741824 | bytes 6815744 | tf_op jit(solution)/shard_map/dot_general | solution.py:85
  178.9 4.5 %fusion.7 = bf16[256,2048]{1,0:T(8,128)(2,1)} fusion(f32[256,2048]{1,0:T(8,128)S(1)} %fusion, bf16[256,1024]{1,0:T(8,128)(2,1)S(1)} %copy-done.4, bf16[3,2048,1024]{2,1,0:T(8,128)(2,1)} %all-gather.2.cloned.1.call-done), kind=kOutput, calls=%fused_computation.16 | convolution fusion | flops 1074790400 | bytes 7864320 | tf_op jit(solution)/shard_map/dot_general | solution.py:87
  183.4 14.9 %all-to-all-done.1 = bf16[8,32,2048]{2,1,0:T(8,128)(2,1)S(1)} async-done(((bf16[8,32,2048]{2,1,0:T(8,128)(2,1)}), bf16[8,32,2048]{2,1,0:T(8,128)(2,1)S(1)}, u32[]{:S(2)}, u32[]{:S(2)}) %all-to-all-start.1) | async-done | bytes 1048608 | tf_op jit(solution)/shard_map/all_to_all | solution.py:121
  198.3 3.6 %all-to-all-start.3 = ((bf16[8,32,2048]{2,1,0:T(8,128)(2,1)}), bf16[8,32,2048]{2,1,0:T(8,128)(2,1)S(1)}, u32[]{:S(2)}, u32[]{:S(2)}) async-start(bf16[8,32,2048]{2,1,0:T(8,128)(2,1)} %bitcast.110), calls=%async_computation.3 | async-start | bytes 2097152 | tf_op jit(solution)/shard_map/all_to_all | solution.py:141
  201.8 0.5 fusion.9
  202.4 3.6 %fusion.18 = f32[1,128,8]{2,0,1:T(1,128)S(1)} fusion(f32[256,1,1]{0,1,2:T(1,128)S(1)} %bitcast.115, s32[128,8]{1,0:T(8,128)S(1)} %copy.59), kind=kOutput, calls=%fused_computation.42 | convolution fusion | flops 3407872 | bytes 9216 | tf_op jit(solution)/shard_map/tks,s->tk/dot_general | solution.py:128
  206.0 0.1 copy.67
  206.2 0.5 fusion.12
  206.7 0.1 copy-done.11
  206.8 0.8 copy.86
  207.6 16.8 %all-to-all-done.3 = bf16[8,32,2048]{2,1,0:T(8,128)(2,1)S(1)} async-done(((bf16[8,32,2048]{2,1,0:T(8,128)(2,1)}), bf16[8,32,2048]{2,1,0:T(8,128)(2,1)S(1)}, u32[]{:S(2)}, u32[]{:S(2)}) %all-to-all-start.3) | async-done | bytes 1048608 | tf_op jit(solution)/shard_map/all_to_all | solution.py:141
  224.4 6.8 %all-to-all-start.4 = ((bf16[16,128,64]{1,2,0:T(8,128)(2,1)}), bf16[16,128,64]{1,2,0:T(8,128)(2,1)S(1)}, u32[]{:S(2)}, u32[]{:S(2)}) async-start(bf16[16,128,64]{1,2,0:T(8,128)(2,1)} %bitcast.98), calls=%async_computation.4 | async-start | bytes 524288 | tf_op jit(solution)/shard_map/all_to_all | solution.py:30
  231.2 0.3 fusion.44
  231.5 1.9 fusion.14
  233.4 0.6 multiply_multiply_fusion
  234.1 1.1 fusion.15
  235.2 5.1 %all-to-all-done.4 = bf16[16,128,64]{1,2,0:T(8,128)(2,1)S(1)} async-done(((bf16[16,128,64]{1,2,0:T(8,128)(2,1)}), bf16[16,128,64]{1,2,0:T(8,128)(2,1)S(1)}, u32[]{:S(2)}, u32[]{:S(2)}) %all-to-all-start.4) | async-done | bytes 262176 | tf_op jit(solution)/shard_map/all_to_all | solution.py:30
  240.3 0.7 broadcast_in_dim.44
  241.0 3.4 %all-to-all-start.5 = ((bf16[8,128,64]{1,2,0:T(8,128)(2,1)}), bf16[8,128,64]{1,2,0:T(8,128)(2,1)S(1)}, u32[]{:S(2)}, u32[]{:S(2)}) async-start(bf16[8,128,64]{1,2,0:T(8,128)(2,1)} %broadcast_in_dim.44), calls=%async_computation.5 | async-start | bytes 262144 | tf_op jit(solution)/shard_map/all_to_all | solution.py:36
  244.4 1.4 convolution_convert_fusion.5
  245.8 72.5 %psum.7 = f32[2048]{0:T(1024)} all-reduce(f32[2048]{0:T(1024)S(1)} %get-tuple-element.42), channel_id=1, replica_groups=mesh['dp'=16,'expert'=8] {'dp','expert'}, use_global_device_ids=true, to_apply=%region_12.13 | all-reduce | flops 2048 | bytes 16384 | tf_op jit(solution)/shard_map/psum | solution.py:162
  318.3 0.6 convert_reduce_fusion.1
  318.9 1.2 fusion.43
  320.1 0.2 copy.73
  320.3 0.9 copy.64
  321.1 0.2 copy.72
  321.3 0.9 copy.63
  322.1 0.2 copy.71
  322.3 0.9 copy.62
  (53 shorter events, 0.5 us)
Async XLA Ops:
  7.2 61.8 %copy-start = (bf16[128,2048]{1,0:T(8,128)(2,1)S(1)}, bf16[128,2048]{1,0:T(8,128)(2,1)}, u32[]{:S(2)}) copy-start(bf16[128,2048]{1,0:T(8,128)(2,1)} %param.15) | copy-start | bytes 1572868
  7.2 60.9 %copy-start.13 = (s32[128,8]{0,1:T(8,128)S(1)}, s32[128,8]{0,1:T(8,128)}, u32[]{:S(2)}) copy-start(s32[128,8]{0,1:T(8,128)} %param.11) | copy-start | bytes 12292
  7.2 60.5 %copy-start.1 = (bf16[128,2048]{1,0:T(8,128)(2,1)S(1)}, bf16[128,2048]{1,0:T(8,128)(2,1)}, u32[]{:S(2)}) copy-start(bf16[128,2048]{1,0:T(8,128)(2,1)} %param.8) | copy-start | bytes 1572868
  7.2 60.5 %copy-start.12 = (f32[2048]{0:T(1024)S(1)}, f32[2048]{0:T(1024)}, u32[]{:S(2)}) copy-start(f32[2048]{0:T(1024)} %param.9) | copy-start | bytes 24580
  7.2 18.7 %copy-start.14 = (bf16[128,64]{0,1:T(8,128)(2,1)S(1)}, bf16[128,64]{0,1:T(8,128)(2,1)}, u32[]{:S(2)}) copy-start(bf16[128,64]{0,1:T(8,128)(2,1)} %param.10) | copy-start | bytes 49156
  7.2 101.3 %all-gather.2.cloned.1.call-start = ((), (), s32[]{:S(2)}) async-start(), calls=%async_computation.7 | async-start | bytes 13369344 | tf_op jit(solution)/shard_map/all_gather | solution.py:15
  15.9 10.0 %copy-start.17 = (f32[128]{0:T(128)}, f32[128]{0:T(128)S(1)}, u32[]{:S(2)}) copy-start(f32[128]{0:T(128)S(1)} %fusion.16) | copy-start | bytes 1540
  15.9 190.3 %copy-start.15 = (f32[128]{0:T(128)}, f32[128]{0:T(128)S(1)}, u32[]{:S(2)}) copy-start(f32[128]{0:T(128)S(1)} %fusion.34) | copy-start | bytes 1540
  18.4 52.6 %all-to-all-start = ((bf16[8,32,2048]{2,1,0:T(8,128)(2,1)}), bf16[8,32,2048]{2,1,0:T(8,128)(2,1)S(1)}, u32[]{:S(2)}, u32[]{:S(2)}) async-start(bf16[8,32,2048]{2,1,0:T(8,128)(2,1)} %bitcast.3), calls=%async_computation | async-start | bytes 2097152 | tf_op jit(solution)/shard_map/all_to_all | solution.py:114
  67.0 0.7 copy-start.2
  69.0 2.1 copy-start.9
  71.1 46.3 %all-to-all-start.2 = ((bf16[8,32,2048]{2,1,0:T(8,128)(2,1)}), bf16[8,32,2048]{2,1,0:T(8,128)(2,1)S(1)}, u32[]{:S(2)}, u32[]{:S(2)}) async-start(bf16[8,32,2048]{2,1,0:T(8,128)(2,1)} %bitcast.109), calls=%async_computation.2 | async-start | bytes 2097152 | tf_op jit(solution)/shard_map/all_to_all | solution.py:135
  77.9 241.0 %reduce-scatter.4.cloned.1.call-start = ((), (), s32[]{:S(2)}) async-start(), calls=%async_computation.8 | async-start | bytes 13369344
  121.7 1.4 copy-start.7
  121.7 1.4 copy-start.3
  121.7 2.7 copy-start.5
  163.5 1.0 copy-start.8
  164.6 10.7 %copy-start.6 = (bf16[256,1024]{1,0:T(8,128)(2,1)S(1)}, bf16[256,1024]{1,0:T(8,128)(2,1)}, u32[]{:S(2)}) copy-start(bf16[256,1024]{1,0:T(8,128)(2,1)} %copy-done.5) | copy-start | bytes 1572868
  169.2 29.1 %all-to-all-start.1 = ((bf16[8,32,2048]{2,1,0:T(8,128)(2,1)}), bf16[8,32,2048]{2,1,0:T(8,128)(2,1)S(1)}, u32[]{:S(2)}, u32[]{:S(2)}) async-start(bf16[8,32,2048]{2,1,0:T(8,128)(2,1)} %bitcast.8), calls=%async_computation.1 | async-start | bytes 2097152 | tf_op jit(solution)/shard_map/all_to_all | solution.py:121
  175.3 3.5 %copy-start.4 = (bf16[256,1024]{1,0:T(8,128)(2,1)S(1)}, bf16[256,1024]{1,0:T(8,128)(2,1)}, u32[]{:S(2)}) copy-start(bf16[256,1024]{1,0:T(8,128)(2,1)} %copy-done.3) | copy-start | bytes 1572868
  198.3 26.1 %all-to-all-start.3 = ((bf16[8,32,2048]{2,1,0:T(8,128)(2,1)}), bf16[8,32,2048]{2,1,0:T(8,128)(2,1)S(1)}, u32[]{:S(2)}, u32[]{:S(2)}) async-start(bf16[8,32,2048]{2,1,0:T(8,128)(2,1)} %bitcast.110), calls=%async_computation.3 | async-start | bytes 2097152 | tf_op jit(solution)/shard_map/all_to_all | solution.py:141
  206.2 0.6 copy-start.11
  224.4 15.9 %all-to-all-start.4 = ((bf16[16,128,64]{1,2,0:T(8,128)(2,1)}), bf16[16,128,64]{1,2,0:T(8,128)(2,1)S(1)}, u32[]{:S(2)}, u32[]{:S(2)}) async-start(bf16[16,128,64]{1,2,0:T(8,128)(2,1)} %bitcast.98), calls=%async_computation.4 | async-start | bytes 524288 | tf_op jit(solution)/shard_map/all_to_all | solution.py:30
  231.2 2.9 copy-start.16
  231.5 12.9 %copy-start.10 = (f32[128,1,256]{2,1,0:T(1,128)S(1)}, f32[128,1,256]{2,1,0:T(1,128)}, u32[]{:S(2)}) copy-start(f32[128,1,256]{2,1,0:T(1,128)} %copy-done.9) | copy-start | bytes 393220
  241.0 77.3 %all-to-all-start.5 = ((bf16[8,128,64]{1,2,0:T(8,128)(2,1)}), bf16[8,128,64]{1,2,0:T(8,128)(2,1)S(1)}, u32[]{:S(2)}, u32[]{:S(2)}) async-start(bf16[8,128,64]{1,2,0:T(8,128)(2,1)} %broadcast_in_dim.44), calls=%async_computation.5 | async-start | bytes 262144 | tf_op jit(solution)/shard_map/all_to_all | solution.py:36
Sparse Core Ops, SparseCore 0:
  9.7 98.7 all-gather.1
  163.7 106.8 reduce-scatter.3
where the time goes:
time: 331 us; the launch traced here: 330 us
  blocking collectives  114 us (34%)
  waiting for transfers between devices  67.2 us (20%)
  matrix products  43.8 us (13%)
  starting transfers between devices  34.4 us (10%)
  other arithmetic  30.8 us (9%)
  local copies, waits for them, and re-layouts  25.9 us (8%)
  between operations  14.4 us (4%)
    psum x1, blocking collectives, body(): gain_sum = lax.psum(grad_gain, ('dp', 'expert'))  72.5 us
    all_gather x1, blocking collectives, body(): router_full = lax.all_gather(router_weight, 'dp', axis=0, tiled=True)  41 us
    all_gather x1, waiting for transfers between devices, in_one_piece(): lax.all_gather(both, axis, axis=dim, tiled=True)  30.4 us
    unnamed x44, local copies, waits for them, and re-layouts  22.4 us
    concatenate x1, other arithmetic, body(): jnp.concatenate([term_gate, term_upper, term_down], axis=1)  21.2 us
    all_to_all x1, waiting for transfers between devices, body(): lax.all_to_all(grad_rows.reshape(window, CAP, D), 'expert', split_axis=0,...  16.8 us
    all_to_all x1, waiting for transfers between devices, body(): lax.all_to_all(produced, 'expert', split_axis=0, concat_axis=0, tiled=True)  14.9 us
    all_to_all x1, starting transfers between devices, body(): lax.all_to_all(outgoing, 'expert', split_axis=0, concat_axis=0, tiled=True)  7.46 us
  transfers between devices with their start and end apart: 8, of which 4 were waited for; matrix products, arithmetic and copies ran while one was open for 14% of the time, Pallas kernels for 0%

commit v1 on v0

--- a/solution.py
+++ b/solution.py
@@ -8,6 +8,11 @@
 CAP = 32
 EPSILON = 1e-05
 HIGHEST = lax.Precision.HIGHEST
+
+
+def gather_and_add(x, name):
+    parts = lax.all_gather(x, name)
+    return jnp.sum(parts, axis=0)
 
 
 def in_one_piece(arrays, axis, dim, along):
@@ -159,7 +164,7 @@
     grad_router = jnp.dot(hidden.astype(jnp.float32).T, grad_logits, precision=HIGHEST)
     router_part = sum_at_owner(grad_router.astype(jnp.bfloat16), "dp", 0)
     router_mine = over_copies(router_part.astype(jnp.bfloat16), "expert").astype(jnp.float32)
-    gain_sum = lax.psum(grad_gain, ("dp", "expert"))
+    gain_sum = gather_and_add(grad_gain, ("dp", "expert"))
     grad_gate_out = summed[:, :FF].astype(jnp.bfloat16)[None]
     grad_up_out = summed[:, FF : 2 * FF].astype(jnp.bfloat16)[None]
     grad_down_out = summed[:, 2 * FF :].astype(jnp.bfloat16)[None]

time: 331 us -> 573 us (1.73)
  waiting for transfers between devices: 67.2 us -> 366 us
  blocking collectives: 114 us -> 41 us
  matrix products: 43.8 us -> 50.2 us
    all_gather x0 -> x1, waiting for transfers between devices: none -> 231 us  [gather_and_add(): parts = lax.all_gather(x, name)]
    unnamed x3 -> x4, waiting for transfers between devices: 0.03 us -> 79.8 us
    psum x1 -> x0, blocking collectives: 72.5 us -> none  [body(): gain_sum = lax.psum(grad_gain, ('dp', 'expert'))]
    all_to_all x1, waiting for transfers between devices: 16.8 us -> 5.84 us  [body(): lax.all_to_all(grad_rows.reshape(window, CAP, D), 'expert', split_axis=0,...]
    all_to_all x1, waiting for transfers between devices: 14.9 us -> 8.7 us  [body(): lax.all_to_all(produced, 'expert', split_axis=0, concat_axis=0, tiled=True)]
    unnamed x44 -> x46, local copies, waits for them, and re-layouts: 22.4 us -> 22.5 us
  transfers between devices with their start and end apart: 8 -> 9, of which waited for: 4 -> 7; matrix products, arithmetic and copies ran while one was open for 14% -> 16% of each run, Pallas kernels for 0% -> 0%
where the time goes in v1:
time: 573 us; the launch traced here: 569 us
  waiting for transfers between devices  366 us (64%)
  matrix products  50.2 us (9%)
  blocking collectives  41 us (7%)
  starting transfers between devices  35.7 us (6%)
  other arithmetic  33.3 us (6%)
  local copies, waits for them, and re-layouts  28.1 us (5%)
  between operations  14.1 us (2%)
    all_gather x1, waiting for transfers between devices, gather_and_add(): parts = lax.all_gather(x, name)  231 us
    unnamed x4, waiting for transfers between devices  79.8 us
    all_gather x1, blocking collectives, body(): router_full = lax.all_gather(router_weight, 'dp', axis=0, tiled=True)  41 us
    all_gather x1, waiting for transfers between devices, in_one_piece(): lax.all_gather(both, axis, axis=dim, tiled=True)  30.8 us
    unnamed x46, local copies, waits for them, and re-layouts  22.5 us
    concatenate x1, other arithmetic, body(): jnp.concatenate([term_gate, term_upper, term_down], axis=1)  21.1 us
  transfers between devices with their start and end apart: 9, of which 7 were waited for; matrix products, arithmetic and copies ran while one was open for 16% of the time, Pallas kernels for 0%

profile of v1, /device:TPU:1, one launch (start us, length us, event | category | flops | bytes accessed | tf_op | source)
XLA Modules:
  0.0 568.6 jit_solution(4727913301268692788)
XLA Ops:
  7.3 2.2 pad_maximum_fusion.1
  9.5 0.8 copy.56
  10.4 2.3 reduce-window.6
  12.7 0.3 slice_reduce_fusion
  13.0 0.2 reduce-window.9
  13.4 0.7 add_select_fusion
  14.2 0.4 convert_reduce_fusion
  14.6 1.2 fusion.16
  15.9 2.5 convolution_convert_fusion.3
  18.4 7.5 %all-to-all-start = ((bf16[8,32,2048]{2,1,0:T(8,128)(2,1)}), bf16[8,32,2048]{2,1,0:T(8,128)(2,1)S(1)}, u32[]{:S(2)}, u32[]{:S(2)}) async-start(bf16[8,32,2048]{2,1,0:T(8,128)(2,1)} %bitcast.3), calls=%async_computation | async-start | bytes 2097152 | tf_op jit(solution)/shard_map/all_to_all | solution.py:119
  25.9 41.0 %all_gather.10 = bf16[2048,64]{0,1:T(8,128)(2,1)S(1)} all-gather(bf16[128,64]{0,1:T(8,128)(2,1)S(1)} %copy-done.13), channel_id=1, replica_groups=mesh['dp'=16,'expert'=8] {'dp'}, dimensions={0}, use_global_device_ids=true | all-gather | bytes 278528 | tf_op jit(solution)/shard_map/all_gather | solution.py:102
  67.0 0.4 fusion.41
  67.4 0.5 copy-done.14
  68.0 0.7 fusion.19
  68.8 2.1 convolution_convert_fusion.4
  70.8 6.8 %all-to-all-start.2 = ((bf16[8,32,2048]{2,1,0:T(8,128)(2,1)}), bf16[8,32,2048]{2,1,0:T(8,128)(2,1)S(1)}, u32[]{:S(2)}, u32[]{:S(2)}) async-start(bf16[8,32,2048]{2,1,0:T(8,128)(2,1)} %bitcast.106), calls=%async_computation.2 | async-start | bytes 2097152 | tf_op jit(solution)/shard_map/all_to_all | solution.py:140
  77.7 30.8 %all-gather.4.cloned.1.call-done = bf16[3,2048,1024]{2,1,0:T(8,128)(2,1)} async-done(((bf16[3,128,1024]{2,1,0:T(8,128)(2,1)}), bf16[3,2048,1024]{2,1,0:T(8,128)(2,1)}) %all-gather.4.cloned.1.call-update) | async-done | bytes 12582928 | tf_op jit(solution)/shard_map/all_gather | solution.py:20
  108.5 4.4 fusion.3
  112.9 4.4 fusion.1
  117.3 5.3 multiply_convert_fusion
  122.7 0.8 copy-done.7
  123.4 4.5 fusion.8
  128.0 6.1 %all-to-all-start.1 = ((bf16[8,32,2048]{2,1,0:T(8,128)(2,1)}), bf16[8,32,2048]{2,1,0:T(8,128)(2,1)}, u32[]{:S(2)}, u32[]{:S(2)}) async-start(bf16[8,32,2048]{2,1,0:T(8,128)(2,1)} %bitcast.108), calls=%async_computation.1 | async-start | bytes 2097152 | tf_op jit(solution)/shard_map/all_to_all | solution.py:126
  134.1 3.7 fusion
  137.8 4.5 fusion.7
  142.3 8.7 %all-to-all-done.1 = bf16[8,32,2048]{2,1,0:T(8,128)(2,1)} async-done(((bf16[8,32,2048]{2,1,0:T(8,128)(2,1)}), bf16[8,32,2048]{2,1,0:T(8,128)(2,1)}, u32[]{:S(2)}, u32[]{:S(2)}) %all-to-all-start.1) | async-done | bytes 1048608 | tf_op jit(solution)/shard_map/all_to_all | solution.py:126
  151.0 4.2 all-to-all-start.3
  155.2 0.2 all-gather.6.cloned.1.call-start
  155.4 1.2 multiply_divide_fusion
  156.6 1.8 fusion.9
  158.4 4.3 fusion.18
  162.6 0.9 copy.67
  163.5 0.7 fusion.33
  164.2 0.7 fusion.31
  164.9 5.8 %all-to-all-done.3 = bf16[8,32,2048]{2,1,0:T(8,128)(2,1)} async-done(((bf16[8,32,2048]{2,1,0:T(8,128)(2,1)}), bf16[8,32,2048]{2,1,0:T(8,128)(2,1)}, u32[]{:S(2)}, u32[]{:S(2)}) %all-to-all-start.3) | async-done | bytes 1048608 | tf_op jit(solution)/shard_map/all_to_all | solution.py:146
  170.8 1.5 fusion.44
  172.3 3.1 fusion.14
  175.5 1.3 convolution_convert_fusion
  176.8 1.3 convolution_convert_fusion.1
  178.2 1.3 convolution_convert_fusion.2
  179.5 21.1 %pad_maximum_fusion = bf16[2048,3072]{0,1:T(8,128)(2,1)} fusion(bf16[2048,1024]{0,1:T(8,128)(2,1)S(1)} %convolution_convert_fusion, bf16[2048,1024]{0,1:T(8,128)(2,1)S(1)} %convolution_convert_fusion.1, bf16[2048,1024]{0,1:T(8,128)(2,1)S(1)} %convolution_convert_fusion.2), kind=kLoop, calls=%fused_computation | loop fusion | flops 37748736 | bytes 25165824 | tf_op jit(solution)/shard_map/concatenate | solution.py:153
  200.6 16.6 %copy.68 = bf16[2048,3072]{1,0:T(8,128)(2,1)} copy(bf16[2048,3072]{0,1:T(8,128)(2,1)} %pad_maximum_fusion) | data formatting | bytes 25165824
  217.3 0.6 copy-done.16
  217.9 0.5 fusion.12
  218.4 0.8 copy.86
  219.1 7.3 %all-to-all-start.4 = ((bf16[16,128,64]{1,2,0:T(8,128)(2,1)}), bf16[16,128,64]{1,2,0:T(8,128)(2,1)S(1)}, u32[]{:S(2)}, u32[]{:S(2)}) async-start(bf16[16,128,64]{1,2,0:T(8,128)(2,1)} %bitcast.98), calls=%async_computation.4 | async-start | bytes 524288 | tf_op jit(solution)/shard_map/all_to_all | solution.py:35
  226.5 1.1 fusion.15
  227.6 6.1 %all-to-all-done.4 = bf16[16,128,64]{1,2,0:T(8,128)(2,1)S(1)} async-done(((bf16[16,128,64]{1,2,0:T(8,128)(2,1)}), bf16[16,128,64]{1,2,0:T(8,128)(2,1)S(1)}, u32[]{:S(2)}, u32[]{:S(2)}) %all-to-all-start.4) | async-done | bytes 262176 | tf_op jit(solution)/shard_map/all_to_all | solution.py:35
  233.7 0.7 broadcast_in_dim.44
  234.4 3.4 all-to-all-start.5
  237.8 2.7 convolution_convert_fusion.5
  240.5 4.3 all-to-all-done.5
  244.8 0.6 convert_reduce_fusion.1
  245.4 230.7 %all-gather.6.cloned.1.call-done = f32[262144]{0:T(1024)} async-done(((f32[2048]{0:T(1024)}), f32[262144]{0:T(1024)}) %all-gather.6.cloned.1.call-update) | async-done | bytes 1048592 | tf_op jit(solution)/shard_map/all_gather | solution.py:14
  476.0 1.4 reshape.138
  477.4 0.7 reduce_sum.153
  478.1 79.8 %reduce-scatter.4.cloned.1.call-done = bf16[128,3072]{1,0:T(8,128)(2,1)} async-done(((bf16[2048,3072]{1,0:T(8,128)(2,1)}), bf16[128,3072]{1,0:T(8,128)(2,1)}) %reduce-scatter.4.cloned.1.call-update) | async-done | bytes 786448
  557.9 1.2 fusion.43
  559.0 0.2 copy.73
  559.2 0.9 copy.64
  560.1 0.2 copy.72
  560.2 0.9 copy.63
  561.1 0.2 copy.71
  561.3 0.9 copy.62
  (59 shorter events, 1.0 us)
Async XLA Ops:
  7.2 61.6 %copy-start = (bf16[128,2048]{1,0:T(8,128)(2,1)S(1)}, bf16[128,2048]{1,0:T(8,128)(2,1)}, u32[]{:S(2)}) copy-start(bf16[128,2048]{1,0:T(8,128)(2,1)} %param.15) | copy-start | bytes 1572868
  7.2 60.2 %copy-start.12 = (s32[128,8]{0,1:T(8,128)S(1)}, s32[128,8]{0,1:T(8,128)}, u32[]{:S(2)}) copy-start(s32[128,8]{0,1:T(8,128)} %param.11) | copy-start | bytes 12292
  7.2 59.8 %copy-start.2 = (bf16[128,2048]{1,0:T(8,128)(2,1)S(1)}, bf16[128,2048]{1,0:T(8,128)(2,1)}, u32[]{:S(2)}) copy-start(bf16[128,2048]{1,0:T(8,128)(2,1)} %param.8) | copy-start | bytes 1572868
  7.2 59.8 %copy-start.11 = (f32[2048]{0:T(1024)S(1)}, f32[2048]{0:T(1024)}, u32[]{:S(2)}) copy-start(f32[2048]{0:T(1024)} %param.9) | copy-start | bytes 24580
  7.2 18.7 %copy-start.13 = (bf16[128,64]{0,1:T(8,128)(2,1)S(1)}, bf16[128,64]{0,1:T(8,128)(2,1)}, u32[]{:S(2)}) copy-start(bf16[128,64]{0,1:T(8,128)(2,1)} %param.10) | copy-start | bytes 49156
  7.2 101.3 %all-gather.4.cloned.1.call-start = ((), (), s32[]{:S(2)}) async-start(), calls=%async_computation.7 | async-start | bytes 13369344 | tf_op jit(solution)/shard_map/all_gather | solution.py:20
  15.9 10.0 %copy-start.17 = (f32[128]{0:T(128)}, f32[128]{0:T(128)S(1)}, u32[]{:S(2)}) copy-start(f32[128]{0:T(128)S(1)} %fusion.16) | copy-start | bytes 1540
  15.9 51.1 %copy-start.15 = (f32[128]{0:T(128)}, f32[128]{0:T(128)S(1)}, u32[]{:S(2)}) copy-start(f32[128]{0:T(128)S(1)} %fusion.34) | copy-start | bytes 1540
  18.4 52.4 %all-to-all-start = ((bf16[8,32,2048]{2,1,0:T(8,128)(2,1)}), bf16[8,32,2048]{2,1,0:T(8,128)(2,1)S(1)}, u32[]{:S(2)}, u32[]{:S(2)}) async-start(bf16[8,32,2048]{2,1,0:T(8,128)(2,1)} %bitcast.3), calls=%async_computation | async-start | bytes 2097152 | tf_op jit(solution)/shard_map/all_to_all | solution.py:119
  67.4 0.5 copy-start.14
  68.7 2.1 copy-start.9
  70.8 46.5 %all-to-all-start.2 = ((bf16[8,32,2048]{2,1,0:T(8,128)(2,1)}), bf16[8,32,2048]{2,1,0:T(8,128)(2,1)S(1)}, u32[]{:S(2)}, u32[]{:S(2)}) async-start(bf16[8,32,2048]{2,1,0:T(8,128)(2,1)} %bitcast.106), calls=%async_computation.2 | async-start | bytes 2097152 | tf_op jit(solution)/shard_map/all_to_all | solution.py:140
  122.7 0.8 copy-start.7
  128.0 23.0 %all-to-all-start.1 = ((bf16[8,32,2048]{2,1,0:T(8,128)(2,1)}), bf16[8,32,2048]{2,1,0:T(8,128)(2,1)}, u32[]{:S(2)}, u32[]{:S(2)}) async-start(bf16[8,32,2048]{2,1,0:T(8,128)(2,1)} %bitcast.108), calls=%async_computation.1 | async-start | bytes 2097152 | tf_op jit(solution)/shard_map/all_to_all | solution.py:126
  134.1 3.7 copy-start.5
  151.0 19.8 %all-to-all-start.3 = ((bf16[8,32,2048]{2,1,0:T(8,128)(2,1)}), bf16[8,32,2048]{2,1,0:T(8,128)(2,1)}, u32[]{:S(2)}, u32[]{:S(2)}) async-start(bf16[8,32,2048]{2,1,0:T(8,128)(2,1)} %bitcast.107), calls=%async_computation.3 | async-start | bytes 2097152 | tf_op jit(solution)/shard_map/all_to_all | solution.py:146
  155.2 320.8 %all-gather.6.cloned.1.call-start = ((), (), s32[]{:S(2)}) async-start(), calls=%async_computation.8 | async-start | bytes 1056768 | tf_op jit(solution)/shard_map/all_gather | solution.py:14
  158.4 17.1 %copy-start.8 = (bf16[256,1024]{1,0:T(8,128)(2,1)S(1)}, bf16[256,1024]{1,0:T(8,128)(2,1)}, u32[]{:S(2)}) copy-start(bf16[256,1024]{1,0:T(8,128)(2,1)} %copy-done.7) | copy-start | bytes 1572868
  175.4 382.4 %reduce-scatter.4.cloned.1.call-start = ((), (), s32[]{:S(2)}) async-start(), calls=%async_computation.9 | async-start | bytes 13369344
  175.5 1.3 copy-start.6
  176.8 1.3 copy-start.4
  217.2 0.7 copy-start.16
  217.2 9.3 %copy-start.18 = (f32[128]{0:T(128)S(1)}, f32[128]{0:T(128)}, u32[]{:S(2)}) copy-start(f32[128]{0:T(128)} %copy-done.17) | copy-start | bytes 1540
  217.2 9.3 %copy-start.3 = (f32[128,2048]{1,0:T(8,128)S(1)}, f32[128,2048]{1,0:T(8,128)}, u32[]{:S(2)}) copy-start(f32[128,2048]{1,0:T(8,128)} %get-tuple-element.50) | copy-start | bytes 3145732
  217.9 19.9 %copy-start.10 = (f32[128,1,256]{2,1,0:T(1,128)S(1)}, f32[128,1,256]{2,1,0:T(1,128)}, u32[]{:S(2)}) copy-start(f32[128,1,256]{2,1,0:T(1,128)} %copy-done.9) | copy-start | bytes 393220
  219.1 14.5 %all-to-all-start.4 = ((bf16[16,128,64]{1,2,0:T(8,128)(2,1)}), bf16[16,128,64]{1,2,0:T(8,128)(2,1)S(1)}, u32[]{:S(2)}, u32[]{:S(2)}) async-start(bf16[16,128,64]{1,2,0:T(8,128)(2,1)} %bitcast.98), calls=%async_computation.4 | async-start | bytes 524288 | tf_op jit(solution)/shard_map/all_to_all | solution.py:35
  234.4 10.4 %all-to-all-start.5 = ((bf16[8,128,64]{1,2,0:T(8,128)(2,1)}), bf16[8,128,64]{1,2,0:T(8,128)(2,1)S(1)}, u32[]{:S(2)}, u32[]{:S(2)}) async-start(bf16[8,128,64]{1,2,0:T(8,128)(2,1)} %broadcast_in_dim.44), calls=%async_computation.5 | async-start | bytes 262144 | tf_op jit(solution)/shard_map/all_to_all | solution.py:41
  237.8 324.3 %copy-start.1 = (bf16[128,2048]{1,0:T(8,128)(2,1)S(1)}, bf16[128,2048]{1,0:T(8,128)(2,1)}, u32[]{:S(2)}) copy-start(bf16[128,2048]{1,0:T(8,128)(2,1)} %param.15) | copy-start | bytes 1572868
Sparse Core Ops, SparseCore 0:
  9.7 98.7 all-gather.3
  175.6 300.4 all-gather.5
  478.5 79.3 reduce-scatter.3
